TPU v7x, 128 devices: a whole 4x4x4 slice. The times are simulated.
128 devices in a mesh: space: 8 (over y_hi, x), dp: 16 (over y_lo, z, core).
Axes of the slice: x: 4, y: 4 (y_hi: 2, y_lo: 2; y = y_hi * 2 + y_lo), z: 4, core: 2. Of those that a mesh axis runs over, the one named last changes fastest.
Arguments:
- mixed_two: bfloat16 [16, 32, 180, 768], P('dp', 'space'), may hold values from -6 to 6
- input_two: bfloat16 [16, 32, 180, 768], P('dp', 'space'), may hold values from -6 to 6
- cotangent: bfloat16 [16, 32, 180, 768], P('dp', 'space'), may hold values from -6 to 6
- w_in_two: bfloat16 [3072, 768], replicated, may hold values from -0.21875 to 0.21875
- w_out_two: bfloat16 [3072, 768], replicated, may hold values from -0.109375 to 0.109375
- kernel_two: bfloat16 [9, 768], replicated, may hold values from -2 to 2
- mixed_one: bfloat16 [16, 32, 180, 768], P('dp', 'space'), may hold values from -6 to 6
- w_in_one: bfloat16 [3072, 768], replicated, may hold values from -0.21875 to 0.21875
- w_out_one: bfloat16 [3072, 768], replicated, may hold values from -0.109375 to 0.109375
- kernel_one: bfloat16 [9, 768], replicated, may hold values from -2 to 2
Outputs:
- input_grad: bfloat16 [16, 32, 180, 768], P('dp', 'space')
- grad_w_in: float32 [3072, 768], P('dp')
- grad_w_out: float32 [3072, 768], P('dp')
- grad_kernel: float32 [9, 768], replicated
All inputs are finite; a program needn't handle non-finite values.
Results may differ from a plain program's by a relative error of at most 0.02.
Values may be sent and summed in bfloat16 or wider, within the bound.
A program may use at most 192 MiB of HBM per device.

v0:
```python
import math

import jax
import jax.numpy as jnp
from jax import lax
from jax.experimental import pallas as pl
from jax.experimental.pallas import tpu as pltpu
from jax.sharding import Mesh
from jax.sharding import PartitionSpec as P

AXES = ("space_0", "space_1", "dp_0", "dp_1", "dp_2")
SPACE = ("space_0", "space_1")
DP = ("dp_0", "dp_1", "dp_2")
MESH = pl.DeviceIdType.MESH
GELU_C = math.sqrt(2.0 / math.pi)
GELU_A = GELU_C * 0.044715
LAST = (((1,), (1,)), ((), ()))
F32 = jnp.float32
BF16 = jnp.bfloat16

D = 768
FF = 3072
LON = 180
PAD = 192
TOK = 4 * PAD
HALF = 2 * PAD
BLK = 384
STEPS = FF // BLK
SUB = 48
GROUPS = 6
LANES = 128
ORDER = (0, 3, 1, 2)
CYCLE = (5, 3, 1, 4, 2, 0)
PERM = tuple(tuple(CYCLE[(g + i) % 6] for i in range(6)) for g in range(GROUPS))


def place_of(group, bits):
    where = 0
    for i, bit in enumerate(PERM[group]):
        where = where + bits[bit] * (1 << (5 - i))
    return where


def gelu_all(v):
    v2 = v * v
    t = jnp.tanh(v * (GELU_C + GELU_A * v2))
    q = 0.5 + 0.5 * t
    slope = q + (v * (1.0 - t * t)) * (0.5 * GELU_C + (1.5 * GELU_A) * v2)
    return v * q, slope


def body(
    mx2_h, in2_h, ct_h, win2_h, wout2_h, k2_h, mx1_h, win1_h, wout1_h, k1_h,
    out_h, gin_h, gout_h, gk_h,
    mx2, ct, mx1, in2, inh, win2, wout2, win1, kt2, kt1,
    pre, slopes, mge, g2, outv, ginv, goutv, kg, kgr,
    stage, d2d, buf, rcv, ag,
    load_sem, d2d_s, d2d_r, rs_s, rs_r, ag_s, ag_r, kg_s, kg_r, halo_s, halo_r, out_sem,
):
    yhi = lax.axis_index("space_0")
    x = lax.axis_index("space_1")
    ylo = lax.axis_index("dp_0")
    z = lax.axis_index("dp_1")
    core = lax.axis_index("dp_2")
    gx1, gx0 = x // 2, (x // 2 + x) % 2
    gz1, gz0 = z // 2, (z // 2 + z) % 2
    near = {
        5: (yhi, 2 * (x // 2) + 1 - x % 2, ylo, z, core),
        4: (yhi, 3 - x, ylo, z, core),
        3: (yhi, x, 1 - ylo, z, core),
        2: (1 - yhi, x, 1 - ylo, z, core),
        1: (yhi, x, ylo, 2 * (z // 2) + 1 - z % 2, core),
        0: (yhi, x, ylo, 3 - z, core),
        "c": (yhi, x, ylo, z, 1 - core),
        "yy": (1 - yhi, x, ylo, z, core),
        "up": ((yhi + x // 3) % 2, (x + 1) % 4, ylo, z, core),
        "down": ((yhi + (3 - x) // 3) % 2, (x + 3) % 4, ylo, z, core),
    }
    first_band = (yhi * 4 + x) == 0
    last_band = (yhi * 4 + x) == 7

    def block_of(s):
        r = 7 - s
        a1, a0, c = r // 4, (r // 2) % 2, r % 2
        z1, z0 = (gz1 + a1) % 2, (gz0 + a0) % 2
        zz = 2 * z1 + (z1 + z0) % 2
        yy = (ylo + c) % 2
        rows = pl.multiple_of((yy * 4 + zz) * BLK, BLK)
        return rows, a1, a0, c

    whole = [
        pltpu.make_async_copy(a, b, load_sem.at[i])
        for i, (a, b) in enumerate(
            ((mx2_h, mx2), (ct_h, ct), (in2_h, in2), (mx1_h, mx1), (win1_h, win1), (k2_h, kt2), (k1_h, kt1))
        )
    ]
    late = pltpu.make_async_copy(wout1_h, wout2, load_sem.at[7])

    def weight_copy(s, which):
        rows = pl.ds(block_of(s)[0], BLK)
        src, dst = ((win2_h, win2), (wout2_h, wout2))[which]
        return pltpu.make_async_copy(src.at[rows], dst.at[rows], load_sem.at[8 + 8 * which + s])

    whole[0].start()
    weight_copy(0, 0).start()
    whole[1].start()
    weight_copy(0, 1).start()

    @pl.loop(1, STEPS)
    def _(s):
        weight_copy(s, 0).start()
        weight_copy(s, 1).start()

    for i in (2, 3, 4, 5, 6):
        whole[i].start()

    barrier = pltpu.get_barrier_semaphore()
    for who in near.values():
        pl.semaphore_signal(barrier, inc=1, device_id=who, device_id_type=MESH)
    pl.semaphore_wait(barrier, len(near))

    def remote(src, dst, ssem, rsem, who):
        return pltpu.make_async_remote_copy(
            src_ref=src, dst_ref=dst, send_sem=ssem, recv_sem=rsem, device_id=near[who], device_id_type=MESH
        )

    def core_copy(s):
        return remote(stage.at[s % 2, 1], d2d.at[s], d2d_s.at[s], d2d_r.at[s], "c")

    def core_add(s):
        rows, a1, a0, c = block_of(s)
        copy = core_copy(s)
        copy.wait_recv()

        @pl.loop(0, 8)
        def _(mq):
            m, q1, q0 = mq // 4, (mq // 2) % 2, mq % 2
            bits = (a1, a0, m, (c + m) % 2, q1, q0)
            for g in range(GROUPS):
                total = stage[s % 2, 0, mq, g].astype(F32) + d2d[s, mq, g].astype(F32)
                buf[g, place_of(g, bits)] = total.astype(BF16)

        copy.wait_send()

    def rs_copy(i, g):
        half = pl.ds(1 << (5 - i), 1 << (5 - i))
        return remote(buf.at[g, half], rcv.at[g, half], rs_s.at[i, g], rs_r.at[i, g], PERM[g][i])

    def rs_send(i):
        for g in range(GROUPS):
            rs_copy(i, g).start()

    def rs_add(i):
        count = 1 << (5 - i)
        for g in range(GROUPS):
            rs_copy(i, g).wait_recv()

        @pl.loop(0, count)
        def _(n):
            for g in range(GROUPS):
                buf[g, n] = (buf[g, n].astype(F32) + rcv[g, count + n].astype(F32)).astype(BF16)

    ag_list = [
        (0, (0, 0, 0), (0, 0, 1), "yy"),
        (1, (1, 0, 0), (1, 0, 1), "yy"),
        (2, (0, 0), (0, 1), 5),
        (3, (1, 0), (1, 2), 4),
        (4, (0, 0), (0, 2), 4),
        (5, (0, 1), (0, 3), 4),
        (6, (1, 0), (1, 1), 5),
        (7, (1, 2), (1, 3), 5),
    ]

    def ag_copy(n):
        _, src, dst, who = ag_list[n]
        return remote(ag.at[src], ag.at[dst], ag_s.at[n], ag_r.at[n], who)

    kg_bits = ("c", 5, 3, 1, 4, 2, 0)

    def kg_copy(t):
        return remote(kg.at[t], kgr.at[t], kg_s.at[t], kg_r.at[t], kg_bits[t])

    def kg_next(t):
        kg_copy(t).wait_recv()
        kg[t + 1] = kg[t] + kgr[t]
        if t + 1 < len(kg_bits):
            kg_copy(t + 1).start()

    halos = [
        remote(in2.at[0], inh.at[1], halo_s.at[0], halo_r.at[0], "down"),
        remote(in2.at[3], inh.at[0], halo_s.at[1], halo_r.at[1], "up"),
        remote(mge.at[1], mge.at[5], halo_s.at[2], halo_r.at[2], "down"),
        remote(mge.at[4], mge.at[0], halo_s.at[3], halo_r.at[3], "up"),
        remote(mge.at[7], mge.at[11], halo_s.at[4], halo_r.at[4], "down"),
        remote(mge.at[10], mge.at[6], halo_s.at[5], halo_r.at[5], "up"),
    ]

    whole[0].wait()
    whole[1].wait()

    @pl.loop(0, STEPS)
    def _(s):
        rows = pl.ds(block_of(s)[0], BLK)
        weight_copy(s, 0).wait()
        weight_copy(s, 1).wait()
        p = lax.dot_general(win2[rows, :], mx2[...], LAST, preferred_element_type=F32)
        h = lax.dot_general(wout2[rows, :], ct[...], LAST, preferred_element_type=F32)
        act, slope = gelu_all(p)
        pg = (h * slope).astype(BF16)
        terms = (
            jnp.dot(pg, mx2[...], preferred_element_type=F32).astype(BF16),
            jnp.dot(act.astype(BF16), ct[...], preferred_element_type=F32).astype(BF16),
        )
        pre[:, rows] = pg.T
        for m in range(2):
            mm = (m + yhi) % 2
            for half in range(2):
                slot = (half + core) % 2
                for q in range(4):
                    qq = ((q // 2 + gx1) % 2) * 2 + (q % 2 + gx0) % 2
                    lo = half * PAD + q * SUB
                    for g in range(GROUPS):
                        stage[s % 2, slot, mm * 4 + qq, g] = terms[m][lo : lo + SUB, g * LANES : (g + 1) * LANES]
        core_copy(s).start()

        @pl.when(s > 0)
        def _():
            core_add(s - 1)

    late.start()
    for i in (2, 3, 4, 5, 6):
        whole[i].wait()
    halos[0].start()
    halos[1].start()

    def mixed_back(src, w, top, base, pair):
        @pl.loop(0, 3)
        def _(nb):
            cols = pl.ds(pl.multiple_of(nb * 256, 256), 256)
            r = jnp.dot(src[top : top + HALF, :], w[:, cols], preferred_element_type=F32).astype(BF16)
            mge[base + pair[0], :, cols] = r[:PAD]
            mge[base + pair[1], :, cols] = r[PAD:]

    mixed_back(pre, win2, 0, 0, (1, 4))
    halos[2].start()
    halos[3].start()
    core_add(STEPS - 1)
    rs_send(0)
    mixed_back(pre, win2, HALF, 0, (2, 3))

    @pl.loop(0, STEPS)
    def _(s):
        rows = pl.ds(pl.multiple_of(s * BLK, BLK), BLK)
        p = lax.dot_general(mx1[...], win1[rows, :], LAST, preferred_element_type=F32)
        slopes[:, rows] = gelu_all(p)[1].astype(BF16)

    def halo_wait(pair, low, high):
        halos[pair].wait_recv()
        halos[pair + 1].wait_recv()

        @pl.when(first_band)
        def _():
            low[...] = jnp.zeros((PAD, D), BF16)

        @pl.when(last_band)
        def _():
            high[...] = jnp.zeros((PAD, D), BF16)

    at_row = lax.broadcasted_iota(jnp.int32, (PAD, LANES), 0)

    def back(v):
        return jnp.where(at_row == LON - 1, v[0:1], pltpu.roll(v, PAD - 1, 0))

    def ahead(v):
        return jnp.where(at_row == 0, v[LON - 1 : LON], pltpu.roll(v, 1, 0))

    halo_wait(0, inh.at[0], inh.at[1])
    halo_wait(2, mge.at[0], mge.at[5])

    kg[0, 8:16] = jnp.zeros((8, D), F32)

    @pl.loop(0, 6)
    def _(lb):
        cols = pl.ds(pl.multiple_of(lb * LANES, LANES), LANES)
        totals = [jnp.zeros((8, LANES), F32) for _ in range(9)]
        for i in range(4):
            v = jnp.where(at_row < LON, mge[i + 1, :, cols].astype(F32), 0.0)
            rolled = (back(v), v, ahead(v))
            for a in range(3):
                e = i + a - 1
                field = inh[0, :, cols] if e < 0 else inh[1, :, cols] if e > 3 else in2[e, :, cols]
                field = field.astype(F32)
                for b in range(3):
                    totals[3 * a + b] += (field * rolled[b]).reshape(PAD // 8, 8, LANES).sum(0)
        for n in range(9):
            kg[0, n : n + 1, cols] = totals[n].sum(0, keepdims=True)

    kg_copy(0).start()

    def mix_transposed(base, kt, get, put):
        @pl.loop(0, 6)
        def _(lb):
            cols = pl.ds(pl.multiple_of(lb * LANES, LANES), LANES)
            taps = kt[:, cols].astype(F32)
            for i in range(4):
                sums = [jnp.zeros((PAD, LANES), F32) for _ in range(3)]
                for a in range(3):
                    v = mge[base + i - a + 2, :, cols].astype(F32)
                    for b in range(3):
                        sums[b] += taps[3 * a + b : 3 * a + b + 1] * v
                put(i, cols, get(i, cols) + sums[1] + back(sums[0]) + ahead(sums[2]))

    def ct_row(i, cols):
        at = ORDER.index(i) * PAD
        return ct[at : at + PAD, cols].astype(F32)

    def g2_row(i, cols):
        at = ORDER.index(i) * PAD
        return g2[at : at + PAD, cols].astype(F32)

    def put_g2(i, cols, v):
        at = ORDER.index(i) * PAD
        g2[at : at + PAD, cols] = jnp.where(at_row < LON, v, 0.0).astype(BF16)

    def put_out(i, cols, v):
        outv[i, :, cols] = v[:LON].astype(BF16)

    mix_transposed(0, kt2, ct_row, put_g2)
    rs_add(0)
    rs_send(1)
    kg_next(0)
    late.wait()

    def hidden_back(top):
        @pl.loop(0, STEPS)
        def _(s):
            rows = pl.ds(pl.multiple_of(s * BLK, BLK), BLK)
            h = lax.dot_general(g2[top : top + HALF, :], wout2[rows, :], LAST, preferred_element_type=F32)
            pre[top : top + HALF, rows] = (h * slopes[top : top + HALF, rows].astype(F32)).astype(BF16)

    hidden_back(0)
    rs_add(1)
    rs_send(2)
    kg_next(1)
    mixed_back(pre, win1, 0, 6, (1, 4))
    halos[4].start()
    halos[5].start()
    rs_add(2)
    rs_send(3)
    kg_next(2)
    hidden_back(HALF)
    rs_add(3)
    rs_send(4)
    kg_next(3)
    mixed_back(pre, win1, HALF, 6, (2, 3))
    rs_add(4)
    rs_send(5)
    kg_next(4)
    halo_wait(4, mge.at[6], mge.at[11])
    mix_transposed(6, kt1, g2_row, put_out)
    out_copy = pltpu.make_async_copy(outv, out_h.at[0], out_sem.at[0])
    out_copy.start()
    rs_add(5)
    kg_next(5)
    for g in range(GROUPS):
        ag[g // 3, 0, 0, g % 3] = buf[g, 0]
    ag_copy(0).start()
    ag_copy(1).start()
    kg_next(6)
    ag_copy(0).wait_recv()
    ag_copy(1).wait_recv()
    ag_copy(2).start()
    ag_copy(3).start()
    ag_copy(2).wait_recv()
    ag_copy(3).wait_recv()
    for n in (4, 5, 6, 7):
        ag_copy(n).start()
    for n in (4, 5, 6, 7):
        ag_copy(n).wait_recv()

    scale = 1.0 / 16.0
    for m, dst in ((0, ginv), (1, goutv)):
        mm = (m + yhi) % 2
        for q in range(4):
            qq = ((q // 2 + gx1) % 2) * 2 + (q % 2 + gx0) % 2
            for g in range(GROUPS):
                dst[q * SUB : (q + 1) * SUB, g * LANES : (g + 1) * LANES] = ag[g // 3, qq, mm, g % 3].astype(F32) * scale
    kg[8] = kg[7] * scale
    outs = [
        pltpu.make_async_copy(ginv, gin_h, out_sem.at[1]),
        pltpu.make_async_copy(goutv, gout_h, out_sem.at[2]),
        pltpu.make_async_copy(kg.at[8], gk_h, out_sem.at[3]),
    ]
    for o in outs:
        o.start()
    for n in range(6):
        halos[n].wait_send()
    for i in range(6):
        for g in range(GROUPS):
            rs_copy(i, g).wait_send()
    for n in range(8):
        ag_copy(n).wait_send()
    for t in range(7):
        kg_copy(t).wait_send()
    out_copy.wait()
    for o in outs:
        o.wait()


def in_rows(a):
    return jnp.pad(a[0], ((0, 0), (0, PAD - LON), (0, 0)))


def in_order(a):
    rows = in_rows(a)
    return jnp.concatenate([rows[i] for i in ORDER], axis=0)


def step(mixed_two, input_two, cotangent, w_in_two, w_out_two, kernel_two, mixed_one, w_in_one, w_out_one, kernel_one):
    dma = pltpu.SemaphoreType.DMA
    vmem = pltpu.VMEM
    tokens = (TOK, D)
    taps = lambda k: jnp.pad(k, ((0, 7), (0, 0)))
    out, gin, gout, gk = pl.pallas_call(
        body,
        out_shape=(
            jax.ShapeDtypeStruct((1, 4, LON, D), BF16),
            jax.ShapeDtypeStruct((PAD, D), F32),
            jax.ShapeDtypeStruct((PAD, D), F32),
            jax.ShapeDtypeStruct((16, D), F32),
        ),
        in_specs=[pl.BlockSpec(memory_space=pl.ANY)] * 10,
        out_specs=[pl.BlockSpec(memory_space=pl.ANY)] * 4,
        scratch_shapes=[
            vmem(tokens, BF16), vmem(tokens, BF16), vmem(tokens, BF16),
            vmem((4, PAD, D), BF16), vmem((2, PAD, D), BF16),
            vmem((FF, D), BF16), vmem((FF, D), BF16), vmem((FF, D), BF16),
            vmem((16, D), BF16), vmem((16, D), BF16),
            vmem((TOK, FF), BF16), vmem((TOK, FF), BF16),
            vmem((12, PAD, D), BF16), vmem(tokens, BF16), vmem((4, LON, D), BF16),
            vmem((PAD, D), F32), vmem((PAD, D), F32),
            vmem((9, 16, D), F32), vmem((7, 16, D), F32),
            vmem((2, 2, 8, GROUPS, SUB, LANES), BF16),
            vmem((STEPS, 8, GROUPS, SUB, LANES), BF16),
            vmem((GROUPS, 64, SUB, LANES), BF16),
            vmem((GROUPS, 64, SUB, LANES), BF16),
            vmem((2, 4, 2, 3, SUB, LANES), BF16),
            dma((24,)), dma((STEPS,)), dma((STEPS,)), dma((6, GROUPS)), dma((6, GROUPS)),
            dma((8,)), dma((8,)), dma((7,)), dma((7,)), dma((6,)), dma((6,)), dma((4,)),
        ],
        compiler_params=pltpu.CompilerParams(
            collective_id=0, has_side_effects=True, vmem_limit_bytes=67000000
        ),
    )(
        in_order(mixed_two), in_rows(input_two), in_order(cotangent), w_in_two, w_out_two, taps(kernel_two),
        in_order(mixed_one), w_in_one, w_out_one, taps(kernel_one),
    )
    return out, gin, gout, gk[:9]


def solution(mesh):
    finer = Mesh(mesh.devices.reshape(2, 4, 2, 4, 2), AXES)
    grid = P(DP, SPACE, None, None)
    return jax.shard_map(
        step,
        mesh=finer,
        in_specs=(grid, grid, grid, P(), P(), P(), grid, P(), P(), P()),
        out_specs=(grid, P(DP, None), P(DP, None), P()),
        check_vma=False,
    )
```

profile of v0, /device:TPU:0, one launch (start us, length us, event | category | flops | bytes accessed | tf_op | source)
XLA Modules:
  0.0 112.9 jit_solution(13832003364685822247)
XLA Ops:
  0.6 1.4 %pad.23.k2_h = bf16[16,768]{1,0:T(8,128)(2,1)} pad(bf16[9,768]{1,0:T(8,128)(2,1)} %param.15, bf16[]{:T(256)} %constant.2.clone.1), padding=0_7x0_0 | pad | bytes 38402 | tf_op jit(solution)/shard_map/jit(_pad)/pad | solution.py:423
  2.0 1.4 %pad.25.k1_h = bf16[16,768]{1,0:T(8,128)(2,1)} pad(bf16[9,768]{1,0:T(8,128)(2,1)} %param.19, bf16[]{:T(256)} %constant.2.clone.1), padding=0_7x0_0 | pad | bytes 38402 | tf_op jit(solution)/shard_map/jit(_pad)/pad | solution.py:423
  3.3 1.4 %copy.26 = bf16[1,4,180,768]{3,2,1,0:T(8,128)(2,1)S(1)} copy(bf16[1,4,180,768]{3,1,2,0:T(4,128)(2,1)} %param.10) | data formatting | bytes 2211840 | tf_op args[0]
  4.7 0.0 copy-start
  4.7 0.1 fusion
  4.8 1.1 %copy-done = bf16[1,4,180,768]{3,1,2,0:T(4,128)(2,1)S(1)} copy-done((bf16[1,4,180,768]{3,1,2,0:T(4,128)(2,1)S(1)}, bf16[1,4,180,768]{3,1,2,0:T(4,128)(2,1)}, u32[]{:S(2)}) %copy-start) | copy-done | bytes 1105944
  5.9 0.1 copy.25
  6.1 0.0 copy-start.1
  6.1 1.1 pad.21.in2_h
  7.2 0.5 copy-done.1
  7.7 0.1 copy.24
  7.9 0.1 fusion.4
  7.9 0.0 copy-start.2
  8.0 1.6 %pad_maximum_fusion = (bf16[768,768]{1,0:T(8,128)(2,1)}, bf16[768,768]{1,0:T(8,128)(2,1)}) fusion(bf16[192,768]{1,0:T(8,128)(2,1)S(1)} %get-tuple-element.27, bf16[192,768]{1,0:T(8,128)(2,1)S(1)} %get-tuple-element.26, bf16[192,768]{1,0:T(8,128)(2,1)S(1)} %get-tuple-element.25, bf16[192,768]{1,0:T(8,128)(2,1)S(1)} %get-tuple-element.24, ...), kind=kLoop, calls=%fused_computation | loop fusion | flops 9437184 | bytes 4718592 | tf_op jit(solution)/shard_map/concatenate | solution.py:416
  9.5 0.1 copy-done.2
  9.6 0.1 copy.23
  9.7 0.1 fusion.8
  9.8 1.1 pad_maximum_fusion.2.mx1_h
  10.9 97.0 %shard_map.129 = (bf16[1,4,180,768]{3,2,1,0:T(8,128)(2,1)}, f32[192,768]{1,0:T(8,128)}, f32[192,768]{1,0:T(8,128)}, f32[16,768]{1,0:T(8,128)}) custom-call(bf16[768,768]{1,0:T(8,128)(2,1)} %get-tuple-element.28.mx2_h, bf16[4,192,768]{2,1,0:T(8,128)(2,1)} %pad.21.in2_h, bf16[768,768]{1,0:T(8,128)(2,1)} %get-tuple-element.29.ct_h, bf16[3072,768]{1,0:T(8,128)(2,1)} %win2_h.1, ...), custom_call_target="tpu_custom_call" | custom-call | tf_op jit(solution)/shard_map/pallas_call | solution.py:424
  107.9 0.0 copy-start.4
  107.9 0.0 copy-start.3
  107.9 2.8 %copy.18 = bf16[1,4,180,768]{3,1,2,0:T(4,128)(2,1)} copy(bf16[1,4,180,768]{3,2,1,0:T(8,128)(2,1)} %get-tuple-element.12) | data formatting | bytes 2211840
  110.7 0.0 copy-done.4
  110.7 0.0 copy-start.5
  110.7 0.8 copy.30
  111.5 0.0 copy-done.3
  111.5 0.8 copy.31
  112.3 0.0 copy-done.5
  112.3 0.6 copy.32
Async XLA Ops:
  4.7 1.2 %copy-start = (bf16[1,4,180,768]{3,1,2,0:T(4,128)(2,1)S(1)}, bf16[1,4,180,768]{3,1,2,0:T(4,128)(2,1)}, u32[]{:S(2)}) copy-start(bf16[1,4,180,768]{3,1,2,0:T(4,128)(2,1)} %param.11) | copy-start | bytes 3317764
  6.1 1.7 %copy-start.1 = (bf16[1,4,180,768]{3,1,2,0:T(4,128)(2,1)S(1)}, bf16[1,4,180,768]{3,1,2,0:T(4,128)(2,1)}, u32[]{:S(2)}) copy-start(bf16[1,4,180,768]{3,1,2,0:T(4,128)(2,1)} %param.12) | copy-start | bytes 3317764
  7.9 1.6 %copy-start.2 = (bf16[1,4,180,768]{3,1,2,0:T(4,128)(2,1)S(1)}, bf16[1,4,180,768]{3,1,2,0:T(4,128)(2,1)}, u32[]{:S(2)}) copy-start(bf16[1,4,180,768]{3,1,2,0:T(4,128)(2,1)} %param.16) | copy-start | bytes 3317764
  107.9 2.8 %copy-start.4 = (f32[192,768]{1,0:T(8,128)S(1)}, f32[192,768]{1,0:T(8,128)}, u32[]{:S(2)}) copy-start(f32[192,768]{1,0:T(8,128)} %get-tuple-element.35) | copy-start | bytes 1769476
  107.9 3.6 %copy-start.3 = (f32[192,768]{1,0:T(8,128)S(1)}, f32[192,768]{1,0:T(8,128)}, u32[]{:S(2)}) copy-start(f32[192,768]{1,0:T(8,128)} %get-tuple-element.36) | copy-start | bytes 1769476
  110.7 1.6 %copy-start.5 = (f32[16,768]{1,0:T(8,128)S(1)}, f32[16,768]{1,0:T(8,128)}, u32[]{:S(2)}) copy-start(f32[16,768]{1,0:T(8,128)} %get-tuple-element.11) | copy-start | bytes 147460
where the time goes:
time: 113 us
  Pallas kernels  97 us (86%)
  local copies, waits for them, and re-layouts  12.5 us (11%)
  other arithmetic  2.68 us (2%)
    pallas_call x1, Pallas kernels, step(): pl.pallas_call(body, out_shape=(jax.ShapeDtypeStruct((1, 4, LON, D), BF16...  97 us
    unnamed x20, local copies, waits for them, and re-layouts  8.48 us
    pad x2, local copies, waits for them, and re-layouts, step(): taps = lambda k: jnp.pad(k, ((0, 7), (0, 0)))  2.7 us
    concatenate x2, other arithmetic, in_order(): return jnp.concatenate([rows[i] for i in ORDER], axis=0)  2.68 us

commit v1 on v0

v1 whole, which is shorter than its diff:
```python
import math

import jax
import jax.numpy as jnp
from jax import lax
from jax.experimental import pallas as pl
from jax.experimental.pallas import tpu as pltpu
from jax.sharding import Mesh
from jax.sharding import PartitionSpec as P

AXES = ("space_0", "space_1", "dp_0", "dp_1", "dp_2")
SPACE = ("space_0", "space_1")
DP = ("dp_0", "dp_1", "dp_2")
MESH = pl.DeviceIdType.MESH
GELU_C = math.sqrt(2.0 / math.pi)
GELU_A = GELU_C * 0.044715
LAST = (((1,), (1,)), ((), ()))
F32 = jnp.float32
BF16 = jnp.bfloat16

D = 768
FF = 3072
LON = 180
PAD = 192
TOK = 4 * PAD
HALF = 2 * PAD
BLK = 384
STEPS = FF // BLK
SUB = 48
TAPS = 9
GROUPS = 6
LANES = 128
VMEM_LIMIT = 44 << 20
SLOTS = 4
ORDER = (0, 3, 1, 2)
PERM = (
    (5, 3, 1, 2, 0, 4),
    (3, 5, 0, 1, 2, 4),
    (1, 4, 3, 0, 2, 5),
    (4, 1, 2, 3, 0, 5),
    (2, 0, 5, 1, 3, 4),
    (0, 2, 4, 3, 1, 5),
)


def place_of(group, bits):
    where = 0
    for i, bit in enumerate(PERM[group]):
        where = where + bits[bit] * (1 << (5 - i))
    return where


def gelu_all(v):
    v2 = v * v
    t = jnp.tanh(v * (GELU_C + GELU_A * v2))
    q = 0.5 + 0.5 * t
    slope = q + (v * (1.0 - t * t)) * (0.5 * GELU_C + (1.5 * GELU_A) * v2)
    return v * q, slope


def body(
    mx2, in2, ct, win2_h, wout2_h, kt2, mx1, win1_h, wout1_h, kt1,
    outv, ginv, goutv, gkv,
    inh, win2, wout2, win1,
    pre, mge, g2, kg, kgr,
    stage, d2d, buf, rcv, ag,
    load_sem, d2d_s, d2d_r, rs_s, rs_r, ag_s, ag_r, kg_s, kg_r, halo_s, halo_r,
):
    yhi = lax.axis_index("space_0")
    x = lax.axis_index("space_1")
    ylo = lax.axis_index("dp_0")
    z = lax.axis_index("dp_1")
    core = lax.axis_index("dp_2")
    gx1, gx0 = x // 2, (x // 2 + x) % 2
    gz1, gz0 = z // 2, (z // 2 + z) % 2
    near = {
        5: (yhi, 2 * (x // 2) + 1 - x % 2, ylo, z, core),
        4: (yhi, 3 - x, ylo, z, core),
        3: (yhi, x, 1 - ylo, z, core),
        2: (1 - yhi, x, 1 - ylo, z, core),
        1: (yhi, x, ylo, 2 * (z // 2) + 1 - z % 2, core),
        0: (yhi, x, ylo, 3 - z, core),
        "c": (yhi, x, ylo, z, 1 - core),
        "yy": (1 - yhi, x, ylo, z, core),
        "up": ((yhi + x // 3) % 2, (x + 1) % 4, ylo, z, core),
        "down": ((yhi + (3 - x) // 3) % 2, (x + 3) % 4, ylo, z, core),
    }
    first_band = (yhi * 4 + x) == 0
    last_band = (yhi * 4 + x) == 7

    def block_of(s):
        r = 7 - s
        a1, a0, c = r // 4, (r // 2) % 2, r % 2
        z1, z0 = (gz1 + a1) % 2, (gz0 + a0) % 2
        zz = 2 * z1 + (z1 + z0) % 2
        yy = (ylo + c) % 2
        rows = pl.multiple_of((yy * 4 + zz) * BLK, BLK)
        return rows, a1, a0, c

    other = pltpu.make_async_copy(win1_h, win1, load_sem.at[16])
    late = pltpu.make_async_copy(wout1_h, wout2, load_sem.at[17])

    def weight_copy(s, which):
        rows = pl.ds(block_of(s)[0], BLK)
        src, dst = ((win2_h, win2), (wout2_h, wout2))[which]
        return pltpu.make_async_copy(src.at[rows], dst.at[rows], load_sem.at[8 * which + s])

    @pl.loop(0, STEPS)
    def _(s):
        weight_copy(s, 0).start()
        weight_copy(s, 1).start()

    other.start()

    barrier = pltpu.get_barrier_semaphore()
    for who in near.values():
        pl.semaphore_signal(barrier, inc=1, device_id=who, device_id_type=MESH)
    pl.semaphore_wait(barrier, len(near))

    def remote(src, dst, ssem, rsem, who):
        return pltpu.make_async_remote_copy(
            src_ref=src, dst_ref=dst, send_sem=ssem, recv_sem=rsem, device_id=near[who], device_id_type=MESH
        )

    def core_copy(s):
        return remote(stage.at[s % 2, 1], d2d.at[s % SLOTS], d2d_s.at[s], d2d_r.at[s], "c")

    def core_add(s):
        rows, a1, a0, c = block_of(s)
        copy = core_copy(s)
        copy.wait_recv()
        for mq in range(8):
            m, q1, q0 = mq // 4, (mq // 2) % 2, mq % 2
            for g in range(GROUPS):
                at = place_of(g, (a1, a0, m, (c + m) % 2, q1, q0))
                buf[g, at] = stage[s % 2, 0, mq, g] + d2d[s % SLOTS, mq, g]
        copy.wait_send()
        first_sends(a1, a0, c)

    def pair_copy(g, a1, a0, c, m, u):
        x1, x0 = (0, u) if PERM[g][5] == 4 else (u, 0)
        at = pl.ds(place_of(g, (a1, a0, m, (c + m) % 2, x1, x0)), 2)
        return remote(buf.at[g, at], rcv.at[g, at], rs_s.at[0, g], rs_r.at[0, g], PERM[g][0])

    def first_sends(a1, a0, c):
        for g in range(GROUPS):
            bit = PERM[g][0]
            if bit in (4, 5):
                for m in range(2):
                    pair_copy(g, a1, a0, c, m, 1).start()
            elif bit in (2, 3):
                for u in range(2):
                    pair_copy(g, a1, a0, c, 1 if bit == 2 else 1 - c, u).start()

        for bit, flag in ((1, a0), (0, a1)):
            g = [p[0] for p in PERM].index(bit)
            if flag == 1:
                for m in range(2):
                    for u in range(2):
                        pair_copy(g, a1, a0, c, m, u).start()

    def rs_copy(i, g):
        half = pl.ds(1 << (5 - i), 1 << (5 - i))
        return remote(buf.at[g, half], rcv.at[g, half], rs_s.at[i, g], rs_r.at[i, g], PERM[g][i])

    def rs_send(i):
        for g in range(GROUPS):
            rs_copy(i, g).start()

    def rs_add(i):
        count = 1 << (5 - i)
        for g in range(GROUPS):
            rs_copy(i, g).wait_recv()

        @pl.loop(0, count)
        def _(n):
            for g in range(GROUPS):
                buf[g, n] = buf[g, n] + rcv[g, count + n]

    ag_list = [
        (0, (0, 0, 0), (0, 0, 1), "yy"),
        (1, (1, 0, 0), (1, 0, 1), "yy"),
        (2, (0, 0), (0, 1), 5),
        (3, (1, 0), (1, 2), 4),
        (4, (0, 0), (0, 2), 4),
        (5, (0, 1), (0, 3), 4),
        (6, (1, 0), (1, 1), 5),
        (7, (1, 2), (1, 3), 5),
    ]

    def ag_copy(n):
        _, src, dst, who = ag_list[n]
        return remote(ag.at[src], ag.at[dst], ag_s.at[n], ag_r.at[n], who)

    kg_bits = ("c", 5, 3, 1, 4, 2, 0)

    def kg_copy(t):
        return remote(kg.at[t], kgr.at[t], kg_s.at[t], kg_r.at[t], kg_bits[t])

    def kg_next(t):
        kg_copy(t).wait_recv()
        kg[t + 1] = kg[t] + kgr[t]
        if t + 1 < len(kg_bits):
            kg_copy(t + 1).start()

    halos = [
        remote(in2.at[0], inh.at[1], halo_s.at[0], halo_r.at[0], "down"),
        remote(in2.at[3], inh.at[0], halo_s.at[1], halo_r.at[1], "up"),
        remote(mge.at[1], mge.at[5], halo_s.at[2], halo_r.at[2], "down"),
        remote(mge.at[4], mge.at[0], halo_s.at[3], halo_r.at[3], "up"),
        remote(mge.at[7], mge.at[11], halo_s.at[4], halo_r.at[4], "down"),
        remote(mge.at[10], mge.at[6], halo_s.at[5], halo_r.at[5], "up"),
    ]

    halos[0].start()
    halos[1].start()

    for s in range(STEPS):
        rows = pl.ds(block_of(s)[0], BLK)
        weight_copy(s, 0).wait()
        weight_copy(s, 1).wait()
        p = lax.dot_general(win2[rows, :], mx2[...], LAST, preferred_element_type=F32)
        h = lax.dot_general(wout2[rows, :], ct[...], LAST, preferred_element_type=F32)
        act, slope = gelu_all(p)
        pg = (h * slope).astype(BF16)
        terms = (
            jnp.dot(pg, mx2[...], preferred_element_type=F32).astype(BF16),
            jnp.dot(act.astype(BF16), ct[...], preferred_element_type=F32).astype(BF16),
        )
        pre[:, rows] = pg.T
        for m in range(2):
            mm = (m + yhi) % 2
            for half in range(2):
                slot = (half + core) % 2
                for q in range(4):
                    qq = ((q // 2 + gx1) % 2) * 2 + (q % 2 + gx0) % 2
                    lo = half * PAD + q * SUB
                    for g in range(GROUPS):
                        stage[s % 2, slot, mm * 4 + qq, g] = terms[m][lo : lo + SUB, g * LANES : (g + 1) * LANES]
        core_copy(s).start()
        if s > 0:
            core_add(s - 1)

    late.start()

    def mixed_back(src, w, top, base, pair):
        @pl.loop(0, 3)
        def _(nb):
            cols = pl.ds(pl.multiple_of(nb * 256, 256), 256)
            r = jnp.dot(src[top : top + HALF, :], w[:, cols], preferred_element_type=F32).astype(BF16)
            mge[base + pair[0], :, cols] = r[:PAD]
            mge[base + pair[1], :, cols] = r[PAD:]

    def halo_wait(pair, low, high):
        halos[pair].wait_recv()
        halos[pair + 1].wait_recv()

        @pl.when(first_band)
        def _():
            low[...] = jnp.zeros((PAD, D), BF16)

        @pl.when(last_band)
        def _():
            high[...] = jnp.zeros((PAD, D), BF16)

    at_row = lax.broadcasted_iota(jnp.int32, (PAD, LANES), 0)

    def back(v):
        return jnp.where(at_row == LON - 1, v[0:1], pltpu.roll(v, PAD - 1, 0))

    def ahead(v):
        return jnp.where(at_row == 0, v[LON - 1 : LON], pltpu.roll(v, 1, 0))

    def kernel_gradient():
        kg[0, 8:16] = jnp.zeros((8, D), F32)

        @pl.loop(0, 6)
        def _(lb):
            cols = pl.ds(pl.multiple_of(lb * LANES, LANES), LANES)
            totals = [jnp.zeros((1, LANES), F32) for _ in range(9)]
            for i in range(4):
                v = jnp.where(at_row < LON, mge[i + 1, :, cols].astype(F32), 0.0)
                rolled = (back(v).astype(BF16), v.astype(BF16), ahead(v).astype(BF16))
                for a in range(3):
                    e = i + a - 1
                    field = inh[0, :, cols] if e < 0 else inh[1, :, cols] if e > 3 else in2[e, :, cols]
                    for b in range(3):
                        term = (field * rolled[b]).reshape(PAD // 16, 16, LANES)
                        part = term[0]
                        for n in range(1, PAD // 16):
                            part = part + term[n]
                        totals[3 * a + b] += part.astype(F32).sum(0, keepdims=True)
            for n in range(9):
                kg[0, n : n + 1, cols] = totals[n]

    def mix_transposed(base, kt, get, put, rows):
        @pl.loop(0, 6)
        def _(lb):
            cols = pl.ds(pl.multiple_of(lb * LANES, LANES), LANES)
            taps = kt[:, cols]
            for i in rows:
                sums = [None] * 3
                for a in range(3):
                    v = mge[base + i - a + 2, :, cols]
                    for b in range(3):
                        term = taps[3 * a + b : 3 * a + b + 1] * v
                        sums[b] = term if a == 0 else sums[b] + term
                sums = [t.astype(F32) for t in sums]
                put(i, cols, get(i, cols) + sums[1] + back(sums[0]) + ahead(sums[2]))

    def ct_row(i, cols):
        at = ORDER.index(i) * PAD
        return ct[at : at + PAD, cols].astype(F32)

    def g2_row(i, cols):
        at = ORDER.index(i) * PAD
        return g2[at : at + PAD, cols].astype(F32)

    def put_g2(i, cols, v):
        at = ORDER.index(i) * PAD
        g2[at : at + PAD, cols] = jnp.where(at_row < LON, v, 0.0).astype(BF16)

    def put_out(i, cols, v):
        outv[0, i, :, cols] = v[:LON].astype(BF16)

    def slopes_one(first, count):
        @pl.loop(first, first + count)
        def _(s):
            rows = pl.ds(pl.multiple_of(s * BLK, BLK), BLK)
            p = lax.dot_general(mx1[...], win1[rows, :], LAST, preferred_element_type=F32)
            pre[:, rows] = gelu_all(p)[1].astype(BF16)

    def hidden_back(top, first, count):
        @pl.loop(first, first + count)
        def _(s):
            rows = pl.ds(pl.multiple_of(s * BLK, BLK), BLK)
            h = lax.dot_general(g2[top : top + HALF, :], wout2[rows, :], LAST, preferred_element_type=F32)
            pre[top : top + HALF, rows] = (h * pre[top : top + HALF, rows].astype(F32)).astype(BF16)

    core_add(STEPS - 1)
    mixed_back(pre, win2, 0, 0, (1, 4))
    rs_add(0)
    rs_send(1)
    halos[2].start()
    halos[3].start()
    mixed_back(pre, win2, HALF, 0, (2, 3))
    other.wait()
    slopes_one(0, 4)
    mix_transposed(0, kt2, ct_row, put_g2, (1, 2))
    rs_add(1)
    rs_send(2)
    slopes_one(4, 4)
    halo_wait(0, inh.at[0], inh.at[1])
    kernel_gradient()
    kg_copy(0).start()
    rs_add(2)
    rs_send(3)
    halo_wait(2, mge.at[0], mge.at[5])
    mix_transposed(0, kt2, ct_row, put_g2, (0, 3))
    late.wait()
    kg_next(0)
    hidden_back(0, 0, 4)
    rs_add(3)
    rs_send(4)
    kg_next(1)
    hidden_back(0, 4, 4)
    rs_add(4)
    rs_send(5)
    kg_next(2)
    mixed_back(pre, win1, 0, 6, (1, 4))
    halos[4].start()
    halos[5].start()
    rs_add(5)
    for g in range(GROUPS):
        ag[g // 3, 0, 0, g % 3] = buf[g, 0]
    ag_copy(0).start()
    ag_copy(1).start()
    kg_next(3)
    hidden_back(HALF, 0, 8)
    kg_next(4)
    mixed_back(pre, win1, HALF, 6, (2, 3))
    kg_next(5)
    ag_copy(0).wait_recv()
    ag_copy(1).wait_recv()
    ag_copy(2).start()
    ag_copy(3).start()
    mix_transposed(6, kt1, g2_row, put_out, (1, 2))
    kg_next(6)
    ag_copy(2).wait_recv()
    ag_copy(3).wait_recv()
    for n in (4, 5, 6, 7):
        ag_copy(n).start()
    halo_wait(4, mge.at[6], mge.at[11])
    mix_transposed(6, kt1, g2_row, put_out, (0, 3))
    for n in (4, 5, 6, 7):
        ag_copy(n).wait_recv()

    scale = 1.0 / 16.0
    for m, dst in ((0, ginv), (1, goutv)):
        mm = (m + yhi) % 2
        for q in range(4):
            qq = ((q // 2 + gx1) % 2) * 2 + (q % 2 + gx0) % 2
            for g in range(GROUPS):
                dst[q * SUB : (q + 1) * SUB, g * LANES : (g + 1) * LANES] = ag[g // 3, qq, mm, g % 3].astype(F32) * scale
    gkv[...] = kg[7, :9] * scale
    for n in range(6):
        halos[n].wait_send()
    for i in range(6):
        for g in range(GROUPS):
            rs_copy(i, g).wait_send()
    for n in range(8):
        ag_copy(n).wait_send()
    for t in range(7):
        kg_copy(t).wait_send()


def in_rows(a):
    return jnp.pad(a[0], ((0, 0), (0, PAD - LON), (0, 0)))


def in_order(a):
    rows = in_rows(a)
    return jnp.concatenate([rows[i] for i in ORDER], axis=0)


def step(mixed_two, input_two, cotangent, w_in_two, w_out_two, kernel_two, mixed_one, w_in_one, w_out_one, kernel_one):
    dma = pltpu.SemaphoreType.DMA
    here, far = pl.BlockSpec(memory_space=pltpu.VMEM), pl.BlockSpec(memory_space=pl.ANY)
    vmem = pltpu.VMEM
    tokens = (TOK, D)
    out, gin, gout, gk = pl.pallas_call(
        body,
        out_shape=(
            jax.ShapeDtypeStruct((1, 4, LON, D), BF16),
            jax.ShapeDtypeStruct((PAD, D), F32),
            jax.ShapeDtypeStruct((PAD, D), F32),
            jax.ShapeDtypeStruct((TAPS, D), F32),
        ),
        in_specs=[here, here, here, far, far, here, here, far, far, here],
        out_specs=[here] * 4,
        scratch_shapes=[
            vmem((2, PAD, D), BF16),
            vmem((FF, D), BF16), vmem((FF, D), BF16), vmem((FF, D), BF16),
            vmem((TOK, FF), BF16),
            vmem((12, PAD, D), BF16), vmem(tokens, BF16),
            vmem((8, 16, D), F32), vmem((7, 16, D), F32),
            vmem((2, 2, 8, GROUPS, SUB, LANES), BF16),
            vmem((SLOTS, 8, GROUPS, SUB, LANES), BF16),
            vmem((GROUPS, 64, SUB, LANES), BF16),
            vmem((GROUPS, 64, SUB, LANES), BF16),
            vmem((2, 4, 2, 3, SUB, LANES), BF16),
            dma((18,)), dma((STEPS,)), dma((STEPS,)), dma((6, GROUPS)), dma((6, GROUPS)),
            dma((8,)), dma((8,)), dma((7,)), dma((7,)), dma((6,)), dma((6,)),
        ],
        compiler_params=pltpu.CompilerParams(
            collective_id=0, has_side_effects=True, vmem_limit_bytes=VMEM_LIMIT
        ),
    )(
        in_order(mixed_two), in_rows(input_two), in_order(cotangent), w_in_two, w_out_two, kernel_two,
        in_order(mixed_one), w_in_one, w_out_one, kernel_one,
    )
    return out, gin, gout, gk


def solution(mesh):
    finer = Mesh(mesh.devices.reshape(2, 4, 2, 4, 2), AXES)
    grid = P(DP, SPACE, None, None)
    return jax.shard_map(
        step,
        mesh=finer,
        in_specs=(grid, grid, grid, P(), P(), P(), grid, P(), P(), P()),
        out_specs=(grid, P(DP, None), P(DP, None), P()),
        check_vma=False,
    )
```

time: 113 us -> 96.4 us (0.85)
  Pallas kernels: 97 us -> 85.4 us
  local copies, waits for them, and re-layouts: 12.5 us -> 9.72 us
  other arithmetic: 2.68 us -> 0.23 us
    pallas_call x1, Pallas kernels: 97 us -> 85.4 us  [step(): pl.pallas_call(body, out_shape=(jax.ShapeDtypeStruct((1, 4, LON, D), BF16...]
    pad x2 -> x0, local copies, waits for them, and re-layouts: 2.7 us -> none  [step(): taps = lambda k: jnp.pad(k, ((0, 7), (0, 0)))]
    concatenate x2, other arithmetic: 2.68 us -> 0.23 us  [in_order(): return jnp.concatenate([rows[i] for i in ORDER], axis=0)]
    pallas_call x0 -> x1, local copies, waits for them, and re-layouts: none -> 1.42 us  [step(): pl.pallas_call(body, out_shape=(jax.ShapeDtypeStruct((1, 4, LON, D), BF16...]
    unnamed x20 -> x17, local copies, waits for them, and re-layouts: 8.48 us -> 7.98 us
where the time goes in v1:
time: 96.4 us; the launch traced here: 96.1 us
  Pallas kernels  85.4 us (89%)
  local copies, waits for them, and re-layouts  9.72 us (10%)
    pallas_call x1, Pallas kernels, step(): pl.pallas_call(body, out_shape=(jax.ShapeDtypeStruct((1, 4, LON, D), BF16...  85.4 us
    unnamed x17, local copies, waits for them, and re-layouts  7.98 us

profile of v1, /device:TPU:0, one launch (start us, length us, event | category | flops | bytes accessed | tf_op | source)
XLA Modules:
  0.0 96.1 jit_solution(8081732865554543148)
XLA Ops:
  0.6 1.4 %copy.26 = bf16[1,4,180,768]{3,2,1,0:T(8,128)(2,1)S(1)} copy(bf16[1,4,180,768]{3,1,2,0:T(4,128)(2,1)} %param.10) | data formatting | bytes 2211840 | tf_op args[0]
  2.0 0.0 copy-start.2
  2.0 0.1 fusion
  2.1 1.1 %copy-done.2 = bf16[1,4,180,768]{3,1,2,0:T(4,128)(2,1)S(1)} copy-done((bf16[1,4,180,768]{3,1,2,0:T(4,128)(2,1)S(1)}, bf16[1,4,180,768]{3,1,2,0:T(4,128)(2,1)}, u32[]{:S(2)}) %copy-start.2) | copy-done | bytes 1105944
  3.2 0.1 copy.25
  3.4 0.0 copy-start.3
  3.4 0.1 pad.14.in2
  3.5 1.1 %copy-done.3 = bf16[1,4,180,768]{3,1,2,0:T(4,128)(2,1)S(1)} copy-done((bf16[1,4,180,768]{3,1,2,0:T(4,128)(2,1)S(1)}, bf16[1,4,180,768]{3,1,2,0:T(4,128)(2,1)}, u32[]{:S(2)}) %copy-start.3) | copy-done | bytes 1105944
  4.6 0.1 copy.24
  4.7 0.1 fusion.4
  4.8 0.0 copy-start.4
  4.8 0.2 pad_maximum_fusion
  5.0 1.1 %copy-done.4 = bf16[1,4,180,768]{3,1,2,0:T(4,128)(2,1)S(1)} copy-done((bf16[1,4,180,768]{3,1,2,0:T(4,128)(2,1)S(1)}, bf16[1,4,180,768]{3,1,2,0:T(4,128)(2,1)}, u32[]{:S(2)}) %copy-start.4) | copy-done | bytes 1105944
  6.1 0.1 copy.23
  6.2 0.1 fusion.8
  6.3 0.0 copy-start
  6.3 0.0 copy-start.1
  6.3 0.1 pad_maximum_fusion.2.mx1
  6.4 0.6 copy-done
  7.0 0.0 copy-done.1
  7.0 85.4 %shard_map.129 = (bf16[1,4,180,768]{3,2,1,0:T(8,128)(2,1)S(1)}, f32[192,768]{1,0:T(8,128)S(1)}, f32[192,768]{1,0:T(8,128)S(1)}, f32[9,768]{1,0:T(8,128)S(1)}) custom-call(bf16[768,768]{1,0:T(8,128)(2,1)S(1)} %get-tuple-element.20.mx2, bf16[4,192,768]{2,1,0:T(8,128)(2,1)S(1)} %pad.14.in2, bf16[768,768]{1,0:T(8,128)(2,1)S(1)} %get-tuple-element.21.ct, ...), custom_call_target="tpu_custom_call" | custom-call | tf_op jit(solution)/shard_map/pallas_call | solution.py:431
  92.4 1.4 %copy.18 = bf16[1,4,180,768]{3,1,2,0:T(4,128)(2,1)} copy(bf16[1,4,180,768]{3,2,1,0:T(8,128)(2,1)S(1)} %get-tuple-element.4) | data formatting | bytes 2211840 | tf_op jit(solution)/shard_map/pallas_call | solution.py:431
  93.8 0.8 copy.30
  94.7 0.8 copy.31
  95.5 0.6 copy.32
Async XLA Ops:
  2.0 1.2 %copy-start.2 = (bf16[1,4,180,768]{3,1,2,0:T(4,128)(2,1)S(1)}, bf16[1,4,180,768]{3,1,2,0:T(4,128)(2,1)}, u32[]{:S(2)}) copy-start(bf16[1,4,180,768]{3,1,2,0:T(4,128)(2,1)} %param.11) | copy-start | bytes 3317764
  3.4 1.2 %copy-start.3 = (bf16[1,4,180,768]{3,1,2,0:T(4,128)(2,1)S(1)}, bf16[1,4,180,768]{3,1,2,0:T(4,128)(2,1)}, u32[]{:S(2)}) copy-start(bf16[1,4,180,768]{3,1,2,0:T(4,128)(2,1)} %param.12) | copy-start | bytes 3317764
  4.8 1.2 %copy-start.4 = (bf16[1,4,180,768]{3,1,2,0:T(4,128)(2,1)S(1)}, bf16[1,4,180,768]{3,1,2,0:T(4,128)(2,1)}, u32[]{:S(2)}) copy-start(bf16[1,4,180,768]{3,1,2,0:T(4,128)(2,1)} %param.16) | copy-start | bytes 3317764
  6.3 0.7 copy-start
  6.3 0.7 copy-start.1

commit v2 on v1

--- a/solution.py
+++ b/solution.py
@@ -50,6 +50,10 @@
     return where
 
 
+def last_bits(group, n):
+    return tuple(sorted(PERM[group][3 + i] for i in range(3) if n & (4 >> i)))
+
+
 def gelu_all(v):
     v2 = v * v
     t = jnp.tanh(v * (GELU_C + GELU_A * v2))
@@ -59,12 +63,12 @@
 
 
 def body(
-    mx2, in2, ct, win2_h, wout2_h, kt2, mx1, win1_h, wout1_h, kt1,
+    mx2, in2, ct, win2_h, wout2_h, k2_h, mx1, win1_h, wout1_h, k1_h,
     outv, ginv, goutv, gkv,
-    inh, win2, wout2, win1,
+    inh, win2, wout2, win1, kt2, kt1,
     pre, mge, g2, kg, kgr,
     stage, d2d, buf, rcv, ag,
-    load_sem, d2d_s, d2d_r, rs_s, rs_r, ag_s, ag_r, kg_s, kg_r, halo_s, halo_r,
+    load_sem, d2d_s, d2d_r, rs_s, rs_r, last_s, last_r, ag_s, ag_r, kg_s, kg_r, halo_s, halo_r,
 ):
     yhi = lax.axis_index("space_0")
     x = lax.axis_index("space_1")
@@ -73,18 +77,35 @@
     core = lax.axis_index("dp_2")
     gx1, gx0 = x // 2, (x // 2 + x) % 2
     gz1, gz0 = z // 2, (z // 2 + z) % 2
+    def flipped(bits):
+        xx, yy_hi, yy_lo, zz = x, yhi, ylo, z
+        if 4 in bits:
+            xx = 3 - xx
+        if 5 in bits:
+            xx = 2 * (xx // 2) + 1 - xx % 2
+        if 0 in bits:
+            zz = 3 - zz
+        if 1 in bits:
+            zz = 2 * (zz // 2) + 1 - zz % 2
+        if 2 in bits:
+            yy_hi, yy_lo = 1 - yy_hi, 1 - yy_lo
+        if 3 in bits:
+            yy_lo = 1 - yy_lo
+        return (yy_hi, xx, yy_lo, zz, core)
+
     near = {
-        5: (yhi, 2 * (x // 2) + 1 - x % 2, ylo, z, core),
-        4: (yhi, 3 - x, ylo, z, core),
-        3: (yhi, x, 1 - ylo, z, core),
-        2: (1 - yhi, x, 1 - ylo, z, core),
-        1: (yhi, x, ylo, 2 * (z // 2) + 1 - z % 2, core),
-        0: (yhi, x, ylo, 3 - z, core),
         "c": (yhi, x, ylo, z, 1 - core),
         "yy": (1 - yhi, x, ylo, z, core),
         "up": ((yhi + x // 3) % 2, (x + 1) % 4, ylo, z, core),
         "down": ((yhi + (3 - x) // 3) % 2, (x + 3) % 4, ylo, z, core),
     }
+    for bit in range(6):
+        near[bit] = flipped((bit,))
+    for g in range(GROUPS):
+        for n in range(1, 8):
+            key = last_bits(g, n)
+            if len(key) > 1 and key not in near:
+                near[key] = flipped(key)
     first_band = (yhi * 4 + x) == 0
     last_band = (yhi * 4 + x) == 7
 
@@ -105,17 +126,18 @@
         src, dst = ((win2_h, win2), (wout2_h, wout2))[which]
         return pltpu.make_async_copy(src.at[rows], dst.at[rows], load_sem.at[8 * which + s])
 
-    @pl.loop(0, STEPS)
-    def _(s):
+    for s in range(2):
         weight_copy(s, 0).start()
         weight_copy(s, 1).start()
 
-    other.start()
+    small = [
+        pltpu.make_async_copy(k2_h, kt2, load_sem.at[18]),
+        pltpu.make_async_copy(k1_h, kt1, load_sem.at[19]),
+    ]
 
     barrier = pltpu.get_barrier_semaphore()
     for who in near.values():
         pl.semaphore_signal(barrier, inc=1, device_id=who, device_id_type=MESH)
-    pl.semaphore_wait(barrier, len(near))
 
     def remote(src, dst, ssem, rsem, who):
         return pltpu.make_async_remote_copy(
@@ -177,6 +199,24 @@
             for g in range(GROUPS):
                 buf[g, n] = buf[g, n] + rcv[g, count + n]
 
+    def last_copy(g, n):
+        key = last_bits(g, n)
+        who = key if len(key) > 1 else key[0]
+        return remote(buf.at[g, n], rcv.at[g, n], last_s.at[g, n], last_r.at[g, n], who)
+
+    def last_send():
+        for n in range(1, 8):
+            for g in range(GROUPS):
+                last_copy(g, n).start()
+
+    def last_add():
+        for g in range(GROUPS):
+            total = buf[g, 0].astype(F32)
+            for n in range(1, 8):
+                last_copy(g, n).wait_recv()
+                total = total + rcv[g, n].astype(F32)
+            ag[g // 3, 0, 0, g % 3] = total.astype(BF16)
+
     ag_list = [
         (0, (0, 0, 0), (0, 0, 1), "yy"),
         (1, (1, 0, 0), (1, 0, 1), "yy"),
@@ -206,19 +246,25 @@
     halos = [
         remote(in2.at[0], inh.at[1], halo_s.at[0], halo_r.at[0], "down"),
         remote(in2.at[3], inh.at[0], halo_s.at[1], halo_r.at[1], "up"),
-        remote(mge.at[1], mge.at[5], halo_s.at[2], halo_r.at[2], "down"),
-        remote(mge.at[4], mge.at[0], halo_s.at[3], halo_r.at[3], "up"),
-        remote(mge.at[7], mge.at[11], halo_s.at[4], halo_r.at[4], "down"),
-        remote(mge.at[10], mge.at[6], halo_s.at[5], halo_r.at[5], "up"),
     ]
-
-    halos[0].start()
-    halos[1].start()
+    for part in range(2):
+        cols = pl.ds(part * (D // 2), D // 2)
+        halos.append(remote(mge.at[1, :, cols], mge.at[5, :, cols], halo_s.at[2 * part + 2], halo_r.at[2 * part + 2], "down"))
+        halos.append(remote(mge.at[4, :, cols], mge.at[0, :, cols], halo_s.at[2 * part + 3], halo_r.at[2 * part + 3], "up"))
+    halos.append(remote(mge.at[7], mge.at[11], halo_s.at[6], halo_r.at[6], "down"))
+    halos.append(remote(mge.at[10], mge.at[6], halo_s.at[7], halo_r.at[7], "up"))
 
     for s in range(STEPS):
         rows = pl.ds(block_of(s)[0], BLK)
         weight_copy(s, 0).wait()
         weight_copy(s, 1).wait()
+        if s + 2 < STEPS:
+            weight_copy(s + 2, 0).start()
+            weight_copy(s + 2, 1).start()
+        else:
+            small[s + 2 - STEPS].start()
+        if s == STEPS - 2:
+            other.start()
         p = lax.dot_general(win2[rows, :], mx2[...], LAST, preferred_element_type=F32)
         h = lax.dot_general(wout2[rows, :], ct[...], LAST, preferred_element_type=F32)
         act, slope = gelu_all(p)
@@ -237,8 +283,13 @@
                     lo = half * PAD + q * SUB
                     for g in range(GROUPS):
                         stage[s % 2, slot, mm * 4 + qq, g] = terms[m][lo : lo + SUB, g * LANES : (g + 1) * LANES]
+        if s == 0:
+            pl.semaphore_wait(barrier, len(near))
         core_copy(s).start()
-        if s > 0:
+        if s == 0:
+            halos[0].start()
+            halos[1].start()
+        else:
             core_add(s - 1)
 
     late.start()
@@ -251,9 +302,9 @@
             mge[base + pair[0], :, cols] = r[:PAD]
             mge[base + pair[1], :, cols] = r[PAD:]
 
-    def halo_wait(pair, low, high):
-        halos[pair].wait_recv()
-        halos[pair + 1].wait_recv()
+    def halo_wait(first, last, low, high):
+        for n in range(first, last):
+            halos[n].wait_recv()
 
         @pl.when(first_band)
         def _():
@@ -345,69 +396,68 @@
     halos[3].start()
     mixed_back(pre, win2, HALF, 0, (2, 3))
     other.wait()
+    for copy in small:
+        copy.wait()
     slopes_one(0, 4)
     mix_transposed(0, kt2, ct_row, put_g2, (1, 2))
     rs_add(1)
     rs_send(2)
+    halos[4].start()
+    halos[5].start()
     slopes_one(4, 4)
-    halo_wait(0, inh.at[0], inh.at[1])
+    halo_wait(0, 2, inh.at[0], inh.at[1])
     kernel_gradient()
     kg_copy(0).start()
     rs_add(2)
-    rs_send(3)
-    halo_wait(2, mge.at[0], mge.at[5])
+    last_send()
+    halo_wait(2, 6, mge.at[0], mge.at[5])
     mix_transposed(0, kt2, ct_row, put_g2, (0, 3))
     late.wait()
     kg_next(0)
-    hidden_back(0, 0, 4)
-    rs_add(3)
-    rs_send(4)
+    hidden_back(0, 0, 8)
     kg_next(1)
-    hidden_back(0, 4, 4)
-    rs_add(4)
-    rs_send(5)
-    kg_next(2)
-    mixed_back(pre, win1, 0, 6, (1, 4))
-    halos[4].start()
-    halos[5].start()
-    rs_add(5)
-    for g in range(GROUPS):
-        ag[g // 3, 0, 0, g % 3] = buf[g, 0]
+    last_add()
     ag_copy(0).start()
     ag_copy(1).start()
+    mixed_back(pre, win1, 0, 6, (1, 4))
+    halos[6].start()
+    halos[7].start()
+    kg_next(2)
+    hidden_back(HALF, 0, 8)
     kg_next(3)
-    hidden_back(HALF, 0, 8)
-    kg_next(4)
-    mixed_back(pre, win1, HALF, 6, (2, 3))
-    kg_next(5)
     ag_copy(0).wait_recv()
     ag_copy(1).wait_recv()
     ag_copy(2).start()
     ag_copy(3).start()
+    mixed_back(pre, win1, HALF, 6, (2, 3))
+    kg_next(4)
     mix_transposed(6, kt1, g2_row, put_out, (1, 2))
-    kg_next(6)
+    kg_next(5)
     ag_copy(2).wait_recv()
     ag_copy(3).wait_recv()
     for n in (4, 5, 6, 7):
         ag_copy(n).start()
-    halo_wait(4, mge.at[6], mge.at[11])
+    halo_wait(6, 8, mge.at[6], mge.at[11])
     mix_transposed(6, kt1, g2_row, put_out, (0, 3))
+    kg_next(6)
     for n in (4, 5, 6, 7):
         ag_copy(n).wait_recv()
 
-    scale = 1.0 / 16.0
     for m, dst in ((0, ginv), (1, goutv)):
         mm = (m + yhi) % 2
         for q in range(4):
             qq = ((q // 2 + gx1) % 2) * 2 + (q % 2 + gx0) % 2
             for g in range(GROUPS):
-                dst[q * SUB : (q + 1) * SUB, g * LANES : (g + 1) * LANES] = ag[g // 3, qq, mm, g % 3].astype(F32) * scale
-    gkv[...] = kg[7, :9] * scale
-    for n in range(6):
+                dst[q * SUB : (q + 1) * SUB, g * LANES : (g + 1) * LANES] = ag[g // 3, qq, mm, g % 3]
+    gkv[...] = kg[7, :TAPS]
+    for n in range(8):
         halos[n].wait_send()
-    for i in range(6):
+    for i in range(3):
         for g in range(GROUPS):
             rs_copy(i, g).wait_send()
+    for g in range(GROUPS):
+        for n in range(1, 8):
+            last_copy(g, n).wait_send()
     for n in range(8):
         ag_copy(n).wait_send()
     for t in range(7):
@@ -432,15 +482,16 @@
         body,
         out_shape=(
             jax.ShapeDtypeStruct((1, 4, LON, D), BF16),
-            jax.ShapeDtypeStruct((PAD, D), F32),
-            jax.ShapeDtypeStruct((PAD, D), F32),
+            jax.ShapeDtypeStruct((PAD, D), BF16),
+            jax.ShapeDtypeStruct((PAD, D), BF16),
             jax.ShapeDtypeStruct((TAPS, D), F32),
         ),
-        in_specs=[here, here, here, far, far, here, here, far, far, here],
+        in_specs=[here, here, here, far, far, far, here, far, far, far],
         out_specs=[here] * 4,
         scratch_shapes=[
             vmem((2, PAD, D), BF16),
             vmem((FF, D), BF16), vmem((FF, D), BF16), vmem((FF, D), BF16),
+            vmem((TAPS, D), BF16), vmem((TAPS, D), BF16),
             vmem((TOK, FF), BF16),
             vmem((12, PAD, D), BF16), vmem(tokens, BF16),
             vmem((8, 16, D), F32), vmem((7, 16, D), F32),
@@ -449,8 +500,8 @@
             vmem((GROUPS, 64, SUB, LANES), BF16),
             vmem((GROUPS, 64, SUB, LANES), BF16),
             vmem((2, 4, 2, 3, SUB, LANES), BF16),
-            dma((18,)), dma((STEPS,)), dma((STEPS,)), dma((6, GROUPS)), dma((6, GROUPS)),
-            dma((8,)), dma((8,)), dma((7,)), dma((7,)), dma((6,)), dma((6,)),
+            dma((20,)), dma((STEPS,)), dma((STEPS,)), dma((3, GROUPS)), dma((3, GROUPS)), dma((GROUPS, 8)), dma((GROUPS, 8)),
+            dma((8,)), dma((8,)), dma((7,)), dma((7,)), dma((8,)), dma((8,)),
         ],
         compiler_params=pltpu.CompilerParams(
             collective_id=0, has_side_effects=True, vmem_limit_bytes=VMEM_LIMIT
@@ -459,7 +510,8 @@
         in_order(mixed_two), in_rows(input_two), in_order(cotangent), w_in_two, w_out_two, kernel_two,
         in_order(mixed_one), w_in_one, w_out_one, kernel_one,
     )
-    return out, gin, gout, gk
+    scale = 1.0 / 16.0
+    return out, gin.astype(F32) * scale, gout.astype(F32) * scale, gk * scale
 
 
 def solution(mesh):

time: 96.4 us -> 87.3 us (0.906)
  Pallas kernels: 85.4 us -> 76.7 us
  local copies, waits for them, and re-layouts: 9.72 us -> 7.54 us
  other arithmetic: 0.23 us -> 1.95 us
    pallas_call x1, Pallas kernels: 85.4 us -> 76.7 us  [step(): pl.pallas_call(body, out_shape=(jax.ShapeDtypeStruct((1, 4, LON, D), BF16...]
    mul x0 -> x2, other arithmetic: none -> 1.71 us  [step(): return (out, gin.astype(F32) * scale, gout.astype(F32) * scale, gk * scale)]
    pallas_call x1 -> x0, local copies, waits for them, and re-layouts: 1.42 us -> none  [step(): pl.pallas_call(body, out_shape=(jax.ShapeDtypeStruct((1, 4, LON, D), BF16...]
    unnamed x17 -> x15, local copies, waits for them, and re-layouts: 7.98 us -> 7.23 us
where the time goes in v2:
time: 87.3 us; the launch traced here: 87 us
  Pallas kernels  76.7 us (88%)
  local copies, waits for them, and re-layouts  7.54 us (9%)
  other arithmetic  1.95 us (2%)
    pallas_call x1, Pallas kernels, step(): pl.pallas_call(body, out_shape=(jax.ShapeDtypeStruct((1, 4, LON, D), BF16...  76.7 us
    unnamed x15, local copies, waits for them, and re-layouts  7.23 us

profile of v2, /device:TPU:0, one launch (start us, length us, event | category | flops | bytes accessed | tf_op | source)
XLA Modules:
  0.0 87.0 jit_solution(575167534597351244)
XLA Ops:
  0.6 1.4 %copy.26 = bf16[1,4,180,768]{3,2,1,0:T(8,128)(2,1)S(1)} copy(bf16[1,4,180,768]{3,1,2,0:T(4,128)(2,1)} %param.10) | data formatting | bytes 2211840 | tf_op args[0]
  2.0 0.1 fusion
  2.1 0.0 copy-start.2
  2.1 0.1 pad_maximum_fusion.mx2
  2.2 1.1 %copy-done.2 = bf16[1,4,180,768]{3,1,2,0:T(4,128)(2,1)S(1)} copy-done((bf16[1,4,180,768]{3,1,2,0:T(4,128)(2,1)S(1)}, bf16[1,4,180,768]{3,1,2,0:T(4,128)(2,1)}, u32[]{:S(2)}) %copy-start.2) | copy-done | bytes 1105944
  3.3 0.1 copy.25
  3.4 0.0 copy-start.3
  3.5 0.1 pad.14.in2
  3.5 1.1 %copy-done.3 = bf16[1,4,180,768]{3,1,2,0:T(4,128)(2,1)S(1)} copy-done((bf16[1,4,180,768]{3,1,2,0:T(4,128)(2,1)S(1)}, bf16[1,4,180,768]{3,1,2,0:T(4,128)(2,1)}, u32[]{:S(2)}) %copy-start.3) | copy-done | bytes 1105944
  4.7 0.1 copy.24
  4.8 0.1 fusion.4
  4.9 0.0 copy-start.4
  4.9 0.1 pad_maximum_fusion.1.ct
  5.0 1.1 %copy-done.4 = bf16[1,4,180,768]{3,1,2,0:T(4,128)(2,1)S(1)} copy-done((bf16[1,4,180,768]{3,1,2,0:T(4,128)(2,1)S(1)}, bf16[1,4,180,768]{3,1,2,0:T(4,128)(2,1)}, u32[]{:S(2)}) %copy-start.4) | copy-done | bytes 1105944
  6.1 0.1 copy.23
  6.3 0.1 fusion.8
  6.3 0.0 copy-start
  6.4 0.0 copy-start.1
  6.4 0.1 pad_maximum_fusion.2.mx1
  6.5 0.6 copy-done
  7.1 0.0 copy-done.1
  7.1 76.7 %shard_map.129 = (bf16[1,4,180,768]{3,2,1,0:T(8,128)(2,1)S(1)}, bf16[192,768]{1,0:T(8,128)(2,1)S(1)}, bf16[192,768]{1,0:T(8,128)(2,1)S(1)}, f32[9,768]{1,0:T(8,128)S(1)}) custom-call(bf16[768,768]{1,0:T(8,128)(2,1)S(1)} %pad_maximum_fusion.mx2, bf16[4,192,768]{2,1,0:T(8,128)(2,1)S(1)} %pad.14.in2, bf16[768,768]{1,0:T(8,128)(2,1)S(1)} %pad_maximum_fusion.1.ct, ...), custom_call_target="tpu_custom_call" | custom-call | tf_op jit(solution)/shard_map/pallas_call | solution.py:481
  83.9 1.4 %copy.18 = bf16[1,4,180,768]{3,1,2,0:T(4,128)(2,1)} copy(bf16[1,4,180,768]{3,2,1,0:T(8,128)(2,1)S(1)} %get-tuple-element.12) | data formatting | bytes 2211840
  85.3 0.6 broadcast_multiply_fusion
  85.9 1.1 %convert_multiply_fusion = (f32[192,768]{1,0:T(8,128)}, f32[192,768]{1,0:T(8,128)}) fusion(bf16[192,768]{1,0:T(8,128)(2,1)S(1)} %get-tuple-element.10, bf16[192,768]{1,0:T(8,128)(2,1)S(1)} %get-tuple-element.9), kind=kLoop, calls=%fused_computation.19 | loop fusion | flops 589824 | bytes 1769472 | tf_op jit(solution)/shard_map/mul | solution.py:514
Async XLA Ops:
  2.1 1.2 %copy-start.2 = (bf16[1,4,180,768]{3,1,2,0:T(4,128)(2,1)S(1)}, bf16[1,4,180,768]{3,1,2,0:T(4,128)(2,1)}, u32[]{:S(2)}) copy-start(bf16[1,4,180,768]{3,1,2,0:T(4,128)(2,1)} %param.11) | copy-start | bytes 3317764
  3.4 1.2 %copy-start.3 = (bf16[1,4,180,768]{3,1,2,0:T(4,128)(2,1)S(1)}, bf16[1,4,180,768]{3,1,2,0:T(4,128)(2,1)}, u32[]{:S(2)}) copy-start(bf16[1,4,180,768]{3,1,2,0:T(4,128)(2,1)} %param.12) | copy-start | bytes 3317764
  4.9 1.2 %copy-start.4 = (bf16[1,4,180,768]{3,1,2,0:T(4,128)(2,1)S(1)}, bf16[1,4,180,768]{3,1,2,0:T(4,128)(2,1)}, u32[]{:S(2)}) copy-start(bf16[1,4,180,768]{3,1,2,0:T(4,128)(2,1)} %param.16) | copy-start | bytes 3317764
  6.3 0.7 copy-start
  6.4 0.7 copy-start.1

commit v3 on v2

--- a/solution.py
+++ b/solution.py
@@ -247,12 +247,12 @@
         remote(in2.at[0], inh.at[1], halo_s.at[0], halo_r.at[0], "down"),
         remote(in2.at[3], inh.at[0], halo_s.at[1], halo_r.at[1], "up"),
     ]
-    for part in range(2):
-        cols = pl.ds(part * (D // 2), D // 2)
-        halos.append(remote(mge.at[1, :, cols], mge.at[5, :, cols], halo_s.at[2 * part + 2], halo_r.at[2 * part + 2], "down"))
-        halos.append(remote(mge.at[4, :, cols], mge.at[0, :, cols], halo_s.at[2 * part + 3], halo_r.at[2 * part + 3], "up"))
-    halos.append(remote(mge.at[7], mge.at[11], halo_s.at[6], halo_r.at[6], "down"))
-    halos.append(remote(mge.at[10], mge.at[6], halo_s.at[7], halo_r.at[7], "up"))
+    for base in (0, 6):
+        for part in range(2):
+            cols = pl.ds(part * (D // 2), D // 2)
+            n = len(halos)
+            halos.append(remote(mge.at[base + 1, :, cols], mge.at[base + 5, :, cols], halo_s.at[n], halo_r.at[n], "down"))
+            halos.append(remote(mge.at[base + 4, :, cols], mge.at[base, :, cols], halo_s.at[n + 1], halo_r.at[n + 1], "up"))
 
     for s in range(STEPS):
         rows = pl.ds(block_of(s)[0], BLK)
@@ -405,11 +405,11 @@
     halos[4].start()
     halos[5].start()
     slopes_one(4, 4)
+    rs_add(2)
+    last_send()
     halo_wait(0, 2, inh.at[0], inh.at[1])
     kernel_gradient()
     kg_copy(0).start()
-    rs_add(2)
-    last_send()
     halo_wait(2, 6, mge.at[0], mge.at[5])
     mix_transposed(0, kt2, ct_row, put_g2, (0, 3))
     late.wait()
@@ -429,6 +429,8 @@
     ag_copy(1).wait_recv()
     ag_copy(2).start()
     ag_copy(3).start()
+    halos[8].start()
+    halos[9].start()
     mixed_back(pre, win1, HALF, 6, (2, 3))
     kg_next(4)
     mix_transposed(6, kt1, g2_row, put_out, (1, 2))
@@ -437,7 +439,7 @@
     ag_copy(3).wait_recv()
     for n in (4, 5, 6, 7):
         ag_copy(n).start()
-    halo_wait(6, 8, mge.at[6], mge.at[11])
+    halo_wait(6, 10, mge.at[6], mge.at[11])
     mix_transposed(6, kt1, g2_row, put_out, (0, 3))
     kg_next(6)
     for n in (4, 5, 6, 7):
@@ -450,7 +452,7 @@
             for g in range(GROUPS):
                 dst[q * SUB : (q + 1) * SUB, g * LANES : (g + 1) * LANES] = ag[g // 3, qq, mm, g % 3]
     gkv[...] = kg[7, :TAPS]
-    for n in range(8):
+    for n in range(10):
         halos[n].wait_send()
     for i in range(3):
         for g in range(GROUPS):
@@ -464,13 +466,11 @@
         kg_copy(t).wait_send()
 
 
-def in_rows(a):
-    return jnp.pad(a[0], ((0, 0), (0, PAD - LON), (0, 0)))
-
-
-def in_order(a):
-    rows = in_rows(a)
-    return jnp.concatenate([rows[i] for i in ORDER], axis=0)
+def fields_in(*fields):
+    every = lax.optimization_barrier(jnp.concatenate([f.transpose(0, 2, 1, 3) for f in fields], axis=0))
+    rows = jnp.pad(every.transpose(0, 2, 1, 3), ((0, 0), (0, 0), (0, PAD - LON), (0, 0)))
+    ordered = [jnp.concatenate([rows[n, i] for i in ORDER], axis=0) for n in range(3)]
+    return ordered[0], ordered[1], ordered[2], rows[3]
 
 
 def step(mixed_two, input_two, cotangent, w_in_two, w_out_two, kernel_two, mixed_one, w_in_one, w_out_one, kernel_one):
@@ -478,6 +478,7 @@
     here, far = pl.BlockSpec(memory_space=pltpu.VMEM), pl.BlockSpec(memory_space=pl.ANY)
     vmem = pltpu.VMEM
     tokens = (TOK, D)
+    mx2, ct, mx1, in2 = fields_in(mixed_two, cotangent, mixed_one, input_two)
     out, gin, gout, gk = pl.pallas_call(
         body,
         out_shape=(
@@ -501,14 +502,13 @@
             vmem((GROUPS, 64, SUB, LANES), BF16),
             vmem((2, 4, 2, 3, SUB, LANES), BF16),
             dma((20,)), dma((STEPS,)), dma((STEPS,)), dma((3, GROUPS)), dma((3, GROUPS)), dma((GROUPS, 8)), dma((GROUPS, 8)),
-            dma((8,)), dma((8,)), dma((7,)), dma((7,)), dma((8,)), dma((8,)),
+            dma((8,)), dma((8,)), dma((7,)), dma((7,)), dma((10,)), dma((10,)),
         ],
         compiler_params=pltpu.CompilerParams(
             collective_id=0, has_side_effects=True, vmem_limit_bytes=VMEM_LIMIT
         ),
     )(
-        in_order(mixed_two), in_rows(input_two), in_order(cotangent), w_in_two, w_out_two, kernel_two,
-        in_order(mixed_one), w_in_one, w_out_one, kernel_one,
+        mx2, in2, ct, w_in_two, w_out_two, kernel_two, mx1, w_in_one, w_out_one, kernel_one,
     )
     scale = 1.0 / 16.0
     return out, gin.astype(F32) * scale, gout.astype(F32) * scale, gk * scale

time: 87.3 us -> 85.8 us (0.983)
  local copies, waits for them, and re-layouts: 7.54 us -> 4.84 us
  other arithmetic: 1.95 us -> 3.2 us
    unnamed x15 -> x9, local copies, waits for them, and re-layouts: 7.23 us -> 2.18 us
    transpose x0 -> x2, local copies, waits for them, and re-layouts: none -> 2.31 us  [fields_in(): f.transpose(0, 2, 1, 3)]
    mul x2 -> x3, other arithmetic: 1.71 us -> 2.33 us  [step(): return (out, gin.astype(F32) * scale, gout.astype(F32) * scale, gk * scale)]
where the time goes in v3:
time: 85.8 us; the launch traced here: 85.3 us
  Pallas kernels  76.6 us (89%)
  local copies, waits for them, and re-layouts  4.84 us (6%)
  other arithmetic  3.2 us (4%)
    pallas_call x1, Pallas kernels, step(): pl.pallas_call(body, out_shape=(jax.ShapeDtypeStruct((1, 4, LON, D), BF16...  76.6 us
    mul x3, other arithmetic, step(): return (out, gin.astype(F32) * scale, gout.astype(F32) * scale, gk * scale)  2.33 us
    transpose x2, local copies, waits for them, and re-layouts, fields_in(): f.transpose(0, 2, 1, 3)  2.31 us
    unnamed x9, local copies, waits for them, and re-layouts  2.18 us

profile of v3, /device:TPU:0, one launch (start us, length us, event | category | flops | bytes accessed | tf_op | source)
XLA Modules:
  0.0 85.3 jit_solution(11709033932115175970)
XLA Ops:
  0.6 0.0 copy-start.3
  0.6 0.0 copy-start.2
  0.7 2.0 %copy_bitcast_fusion.2 = (bf16[1,180,4,768]{3,1,2,0:T(8,128)(2,1)S(1)}, bf16[1,180,4,768]{3,1,2,0:T(8,128)(2,1)S(1)}) fusion(bf16[1,4,180,768]{3,1,2,0:T(4,128)(2,1)} %param.12, bf16[1,4,180,768]{3,1,2,0:T(4,128)(2,1)} %param.10), kind=kLoop, calls=%fused_computation.7 | loop fusion | bytes 4423680 | tf_op jit(solution)/shard_map/transpose | solution.py:470
  2.7 0.0 copy-done.3
  2.7 0.2 copy-done.2
  2.9 0.3 copy_bitcast_fusion
  3.2 0.6 pad_maximum_fusion
  3.8 0.1 slice_bitcast_fusion.2
  3.9 0.1 slice_bitcast_fusion.in2
  4.0 0.2 slice_bitcast_fusion.4
  4.2 0.1 pad_maximum_fusion.3.mx1
  4.3 0.0 copy-start
  4.3 0.0 copy-start.1
  4.3 0.1 pad_maximum_fusion.1.mx2
  4.4 0.1 pad_maximum_fusion.2.ct
  4.5 0.5 copy-done
  5.0 0.0 copy-done.1
  5.0 76.6 %shard_map.129 = (bf16[1,4,180,768]{3,2,1,0:T(8,128)(2,1)S(1)}, bf16[192,768]{1,0:T(8,128)(2,1)S(1)}, bf16[192,768]{1,0:T(8,128)(2,1)S(1)}, f32[9,768]{1,0:T(8,128)S(1)}) custom-call(bf16[768,768]{1,0:T(8,128)(2,1)S(1)} %pad_maximum_fusion.1.mx2, bf16[4,192,768]{2,1,0:T(8,128)(2,1)S(1)} %slice_bitcast_fusion.in2, bf16[768,768]{1,0:T(8,128)(2,1)S(1)} %pad_maximum_fusion.2.ct, ...), custom_call_target="tpu_custom_call" | custom-call | tf_op jit(solution)/shard_map/pallas_call | solution.py:482
  81.6 1.4 %copy.18 = bf16[1,4,180,768]{3,1,2,0:T(4,128)(2,1)} copy(bf16[1,4,180,768]{3,2,1,0:T(8,128)(2,1)S(1)} %get-tuple-element.12) | data formatting | bytes 2211840
  83.0 0.6 broadcast_multiply_fusion
  83.6 0.9 %convert_multiply_fusion.1 = f32[192,768]{1,0:T(8,128)} fusion(bf16[192,768]{1,0:T(8,128)(2,1)S(1)} %get-tuple-element.9), kind=kLoop, calls=%fused_computation.10 | loop fusion | flops 294912 | bytes 884736 | tf_op jit(solution)/shard_map/mul | solution.py:514
  84.5 0.9 %convert_multiply_fusion = f32[192,768]{1,0:T(8,128)} fusion(bf16[192,768]{1,0:T(8,128)(2,1)S(1)} %get-tuple-element.10), kind=kLoop, calls=%fused_computation.9 | loop fusion | flops 294912 | bytes 884736 | tf_op jit(solution)/shard_map/mul | solution.py:514
Async XLA Ops:
  0.6 2.0 %copy-start.3 = (bf16[1,4,180,768]{3,1,2,0:T(4,128)(2,1)S(1)}, bf16[1,4,180,768]{3,1,2,0:T(4,128)(2,1)}, u32[]{:S(2)}) copy-start(bf16[1,4,180,768]{3,1,2,0:T(4,128)(2,1)} %param.16) | copy-start | bytes 3317764
  0.6 2.2 %copy-start.2 = (bf16[1,4,180,768]{3,1,2,0:T(4,128)(2,1)S(1)}, bf16[1,4,180,768]{3,1,2,0:T(4,128)(2,1)}, u32[]{:S(2)}) copy-start(bf16[1,4,180,768]{3,1,2,0:T(4,128)(2,1)} %param.11) | copy-start | bytes 3317764
  4.3 0.7 copy-start
  4.3 0.7 copy-start.1

commit v4 on v3

--- a/solution.py
+++ b/solution.py
@@ -185,29 +185,26 @@
         half = pl.ds(1 << (5 - i), 1 << (5 - i))
         return remote(buf.at[g, half], rcv.at[g, half], rs_s.at[i, g], rs_r.at[i, g], PERM[g][i])
 
-    def rs_send(i):
-        for g in range(GROUPS):
-            rs_copy(i, g).start()
-
-    def rs_add(i):
-        count = 1 << (5 - i)
-        for g in range(GROUPS):
-            rs_copy(i, g).wait_recv()
-
-        @pl.loop(0, count)
-        def _(n):
-            for g in range(GROUPS):
-                buf[g, n] = buf[g, n] + rcv[g, count + n]
-
     def last_copy(g, n):
         key = last_bits(g, n)
         who = key if len(key) > 1 else key[0]
         return remote(buf.at[g, n], rcv.at[g, n], last_s.at[g, n], last_r.at[g, n], who)
 
-    def last_send():
-        for n in range(1, 8):
-            for g in range(GROUPS):
-                last_copy(g, n).start()
+    def rs_step(i):
+        count = 1 << (5 - i)
+        for g in sorted(range(GROUPS), key=lambda n: PERM[n][i] in (4, 5)):
+            rs_copy(i, g).wait_recv()
+
+            @pl.loop(0, count // 4)
+            def _(n):
+                kept, come = pl.ds(n * 4, 4), pl.ds(count + n * 4, 4)
+                buf[g, kept] = buf[g, kept] + rcv[g, come]
+
+            if i < 2:
+                rs_copy(i + 1, g).start()
+            else:
+                for n in range(1, 8):
+                    last_copy(g, n).start()
 
     def last_add():
         for g in range(GROUPS):
@@ -232,7 +229,7 @@
         _, src, dst, who = ag_list[n]
         return remote(ag.at[src], ag.at[dst], ag_s.at[n], ag_r.at[n], who)
 
-    kg_bits = ("c", 5, 3, 1, 4, 2, 0)
+    kg_bits = ("c", 5, 4, 3, 1, 2, 0)
 
     def kg_copy(t):
         return remote(kg.at[t], kgr.at[t], kg_s.at[t], kg_r.at[t], kg_bits[t])
@@ -390,8 +387,7 @@
 
     core_add(STEPS - 1)
     mixed_back(pre, win2, 0, 0, (1, 4))
-    rs_add(0)
-    rs_send(1)
+    rs_step(0)
     halos[2].start()
     halos[3].start()
     mixed_back(pre, win2, HALF, 0, (2, 3))
@@ -400,13 +396,11 @@
         copy.wait()
     slopes_one(0, 4)
     mix_transposed(0, kt2, ct_row, put_g2, (1, 2))
-    rs_add(1)
-    rs_send(2)
+    rs_step(1)
     halos[4].start()
     halos[5].start()
     slopes_one(4, 4)
-    rs_add(2)
-    last_send()
+    rs_step(2)
     halo_wait(0, 2, inh.at[0], inh.at[1])
     kernel_gradient()
     kg_copy(0).start()

time: 85.8 us -> 89.5 us (1.043)
  Pallas kernels: 76.6 us -> 79.8 us
    pallas_call x1, Pallas kernels: 76.6 us -> 79.8 us  [step(): pl.pallas_call(body, out_shape=(jax.ShapeDtypeStruct((1, 4, LON, D), BF16...]
where the time goes in v4:
time: 89.5 us; the launch traced here: 88.6 us
  Pallas kernels  79.8 us (89%)
  local copies, waits for them, and re-layouts  4.84 us (5%)
  other arithmetic  3.2 us (4%)
    pallas_call x1, Pallas kernels, step(): pl.pallas_call(body, out_shape=(jax.ShapeDtypeStruct((1, 4, LON, D), BF16...  79.8 us
    mul x3, other arithmetic, step(): return (out, gin.astype(F32) * scale, gout.astype(F32) * scale, gk * scale)  2.33 us
    transpose x2, local copies, waits for them, and re-layouts, fields_in(): f.transpose(0, 2, 1, 3)  2.31 us
    unnamed x9, local copies, waits for them, and re-layouts  2.18 us

profile of v4, /device:TPU:0, one launch (start us, length us, event | category | flops | bytes accessed | tf_op | source)
XLA Modules:
  0.0 88.6 jit_solution(5982737024289264039)
XLA Ops:
  0.6 0.0 copy-start.3
  0.6 0.0 copy-start.2
  0.7 2.0 %copy_bitcast_fusion.2 = (bf16[1,180,4,768]{3,1,2,0:T(8,128)(2,1)S(1)}, bf16[1,180,4,768]{3,1,2,0:T(8,128)(2,1)S(1)}) fusion(bf16[1,4,180,768]{3,1,2,0:T(4,128)(2,1)} %param.12, bf16[1,4,180,768]{3,1,2,0:T(4,128)(2,1)} %param.10), kind=kLoop, calls=%fused_computation.7 | loop fusion | bytes 4423680 | tf_op jit(solution)/shard_map/transpose | solution.py:464
  2.7 0.0 copy-done.3
  2.7 0.2 copy-done.2
  2.9 0.3 copy_bitcast_fusion
  3.2 0.6 pad_maximum_fusion
  3.8 0.1 slice_bitcast_fusion.2
  3.9 0.1 slice_bitcast_fusion.in2
  4.0 0.2 slice_bitcast_fusion.4
  4.2 0.1 pad_maximum_fusion.3.mx1
  4.3 0.0 copy-start
  4.3 0.0 copy-start.1
  4.3 0.1 pad_maximum_fusion.1.mx2
  4.4 0.1 pad_maximum_fusion.2.ct
  4.5 0.5 copy-done
  5.0 0.0 copy-done.1
  5.0 79.8 %shard_map.129 = (bf16[1,4,180,768]{3,2,1,0:T(8,128)(2,1)S(1)}, bf16[192,768]{1,0:T(8,128)(2,1)S(1)}, bf16[192,768]{1,0:T(8,128)(2,1)S(1)}, f32[9,768]{1,0:T(8,128)S(1)}) custom-call(bf16[768,768]{1,0:T(8,128)(2,1)S(1)} %pad_maximum_fusion.1.mx2, bf16[4,192,768]{2,1,0:T(8,128)(2,1)S(1)} %slice_bitcast_fusion.in2, bf16[768,768]{1,0:T(8,128)(2,1)S(1)} %pad_maximum_fusion.2.ct, ...), custom_call_target="tpu_custom_call" | custom-call | tf_op jit(solution)/shard_map/pallas_call | solution.py:476
  84.9 1.4 %copy.18 = bf16[1,4,180,768]{3,1,2,0:T(4,128)(2,1)} copy(bf16[1,4,180,768]{3,2,1,0:T(8,128)(2,1)S(1)} %get-tuple-element.12) | data formatting | bytes 2211840
  86.3 0.6 broadcast_multiply_fusion
  86.9 0.9 convert_multiply_fusion.1
  87.8 0.9 convert_multiply_fusion
Async XLA Ops:
  0.6 2.0 %copy-start.3 = (bf16[1,4,180,768]{3,1,2,0:T(4,128)(2,1)S(1)}, bf16[1,4,180,768]{3,1,2,0:T(4,128)(2,1)}, u32[]{:S(2)}) copy-start(bf16[1,4,180,768]{3,1,2,0:T(4,128)(2,1)} %param.16) | copy-start | bytes 3317764
  0.6 2.2 %copy-start.2 = (bf16[1,4,180,768]{3,1,2,0:T(4,128)(2,1)S(1)}, bf16[1,4,180,768]{3,1,2,0:T(4,128)(2,1)}, u32[]{:S(2)}) copy-start(bf16[1,4,180,768]{3,1,2,0:T(4,128)(2,1)} %param.11) | copy-start | bytes 3317764
  4.3 0.7 copy-start
  4.3 0.7 copy-start.1
